TPU v7x, 128 devices: a whole 4x4x4 slice. The times are simulated.
128 devices in a mesh: lat: 16 (over x, z), lon: 8 (over y, core).
Axes of the slice: x: 4, y: 4, z: 4, core: 2. Of those that a mesh axis runs over, the one named last changes fastest.
Arguments:
- increment: bfloat16 [32, 16, 144, 128], P('lat', 'lon'), may hold values from -6 to 6
- cotangent: bfloat16 [16, 8, 40, 144, 128], P('lat', 'lon'), may hold values from -6 to 6
- weights: bfloat16 [16, 8, 40, 16, 128, 128], P('lat', 'lon'), may hold values from -0.1875 to 0.1875
- source_ids: int32 [16, 8, 40, 16], P('lat', 'lon'), may hold values from 0 to 511, as said below
- counts: int32 [16, 8, 40], P('lat', 'lon'), may hold values from 0 to 16, as said below
Outputs:
- ocean: bfloat16 [16, 8, 40, 144, 128], P('lat', 'lon')
- atmos_adjoint: bfloat16 [32, 16, 144, 128], P('lat', 'lon')
Inputs may be any that keep to these rules, and one draw needn't show every extreme that they name: source_ids[i, j, t, k] = a * 16 + b with block row a between i * 2 - 1 and (i + 1) * 2, and block column b equal, modulo 16, to one of j * 2 - 1 to (j + 1) * 2. `counts`: every device's tile (i, j) has some target block with exactly 16 live slots.
All inputs are finite; a program needn't handle non-finite values.
Results may differ from a plain program's by a relative error of at most 0.001.
Values may be sent and summed in bfloat16 or wider, within the bound.
No kernel may reach another device: no remote copies, remote signals or barrier semaphores. Data moves between devices by JAX's collectives and lax.ppermute only.
A program may use at most 192 MiB of HBM per device.

v0:
```python
import jax
import jax.numpy as jnp
from jax import lax
from jax.sharding import PartitionSpec as P


def from_behind(value, axis, by):
    peers = lax.axis_size(axis)
    return lax.ppermute(value, axis, [(i, (i + by) % peers) for i in range(peers)])


def passed_along(block, axis, distance):
    devices = range(lax.axis_size(axis))
    route = [(i - distance, i) for i in devices if i - distance in devices]
    return lax.ppermute(block, axis, route)


def with_halo(block, sides, width):
    for axis, dim in sides:
        count = lax.axis_size(axis)
        forward = [(i, i + 1) for i in range(count - 1)]
        forward.append((count - 1, 0))
        backward = [(target, source) for source, target in forward]
        low = lax.ppermute(
            lax.slice_in_dim(block, block.shape[dim] - width, None, axis=dim), axis, forward
        )
        high = lax.ppermute(lax.slice_in_dim(block, 0, width, axis=dim), axis, backward)
        block = jnp.concatenate([low, block, high], axis=dim)
    return block


def fold_lon(partial_value):
    from_west = from_behind(partial_value[:, -1:], "lon", 1)
    from_east = from_behind(partial_value[:, :1], "lon", -1)
    middle = partial_value[:, 1:-1]
    return middle.at[:, :1].add(from_west).at[:, -1:].add(from_east)


def fold_lat(partial_value):
    from_north = passed_along(partial_value[-1:], "lat", 1)
    from_south = passed_along(partial_value[:1], "lat", -1)
    middle = partial_value[1:-1]
    return middle.at[:1].add(from_north).at[-1:].add(from_south)


def body(increment, cotangent, weights, source_ids, counts):
    tile_side = increment.shape[0]
    level_rows = increment.shape[2]
    block_cells = increment.shape[3]
    lon_count = lax.axis_size("lon")
    cycle_blocks = tile_side * lon_count
    lat_index = lax.axis_index("lat")
    lon_index = lax.axis_index("lon")
    source_list = source_ids[0, 0]
    live_counts = counts[0, 0]
    blocks = weights[0, 0]
    cotan_local = cotangent[0, 0]
    slot_count = blocks.shape[1]
    block_row = source_list // cycle_blocks
    block_col = source_list % cycle_blocks
    ext_col = (block_col - lon_index * tile_side + 1 + cycle_blocks) % cycle_blocks
    ext_width = tile_side + 2
    ext_rows = tile_side + 2
    ext_row = block_row - lat_index * tile_side + 1
    ext_total = ext_rows * ext_width
    positions = ext_row * ext_width + ext_col
    slot_index = jnp.arange(slot_count, dtype=jnp.int32)[None, :]
    active = slot_index < live_counts[:, None]
    place_index = jnp.arange(ext_total, dtype=jnp.int32)[None, None, :]
    selector = jnp.logical_and(positions[:, :, None] == place_index, active[:, :, None])
    extended = with_halo(increment, (("lat", 0), ("lon", 1)), 1)
    flattened = extended.reshape(ext_total, level_rows, block_cells)
    picked = jnp.einsum(
        "tke,ews->tkws",
        selector.astype(jnp.bfloat16),
        flattened,
        preferred_element_type=jnp.float32,
    ).astype(jnp.bfloat16)
    ocean_sum = jnp.einsum("tkws,tksb->twb", picked, blocks, preferred_element_type=jnp.float32)
    contribution = jnp.einsum(
        "twb,tksb->tkws", cotan_local, blocks, preferred_element_type=jnp.float32
    )
    partial_value = jnp.einsum(
        "tke,tkws->ews",
        selector.astype(jnp.float32),
        contribution,
        precision=lax.Precision.HIGHEST,
        preferred_element_type=jnp.float32,
    )
    partial_value = partial_value.reshape(ext_rows, ext_width, level_rows, block_cells)
    result_blocks = fold_lat(fold_lon(partial_value))
    return (ocean_sum.astype(jnp.bfloat16)[None, None], result_blocks.astype(jnp.bfloat16))


def solution(mesh):
    placed = (
        P("lat", "lon", None, None),
        P("lat", "lon", None, None, None),
        P("lat", "lon", None, None, None, None),
        P("lat", "lon", None, None),
        P("lat", "lon", None),
    )
    return jax.shard_map(
        body,
        mesh=mesh,
        in_specs=placed,
        out_specs=(P("lat", "lon", None, None, None), P("lat", "lon", None, None)),
        check_vma=False,
    )
```

profile of v0, /device:TPU:15, one launch (start us, length us, event | category | flops | bytes accessed | tf_op | source)
XLA Modules:
  0.0 135.5 jit_solution(15042297549956392149)
XLA Ops:
  0.6 1.7 %fusion.41 = (bf16[1,2,144,128]{3,2,1,0:T(8,128)(2,1)}, bf16[1,2,144,128]{3,2,1,0:T(8,128)(2,1)}) fusion(bf16[2,2,144,128]{3,2,1,0:T(8,128)(2,1)} %param.13), kind=kLoop, calls=%fused_computation.57 | loop fusion | bytes 294912 | tf_op jit(solution)/shard_map/slice | solution.py:27
  2.3 1.6 %collective-permute-start = (bf16[1,2,144,128]{3,2,1,0:T(8,128)(2,1)}, bf16[1,2,144,128]{3,2,1,0:T(8,128)(2,1)}, u32[]{:S(2)}, u32[]{:S(2)}) collective-permute-start(bf16[1,2,144,128]{3,2,1,0:T(8,128)(2,1)} %get-tuple-element.58), channel_id=1, source_target_pairs={{0,8},{8,16},{16,24},{24,32},{32,40},{40,48},{48,56},{56,64},{64,7... | collective-permute-start | bytes 221192 | tf_op jit(solution)/shard_map/ppermute | solution.py:24
  4.0 2.4 %collective-permute-start.1 = (bf16[1,2,144,128]{3,2,1,0:T(8,128)(2,1)}, bf16[1,2,144,128]{3,2,1,0:T(8,128)(2,1)S(1)}, u32[]{:S(2)}, u32[]{:S(2)}) collective-permute-start(bf16[1,2,144,128]{3,2,1,0:T(8,128)(2,1)} %get-tuple-element.57), channel_id=1, source_target_pairs={{8,0},{16,8},{24,16},{32,24},{40,32},{48,40},{56,48},{64,56},{72,6... | collective-permute-start | bytes 221192 | tf_op jit(solution)/shard_map/ppermute | solution.py:27
  6.4 0.7 iota_compare_fusion.1
  7.0 23.1 %fusion.4 = f32[40,16,128,144]{2,3,1,0:T(8,128)} fusion(bf16[1,1,40,16,128,128]{5,4,3,2,1,0:T(8,128)(2,1)} %param.15, bf16[1,1,40,144,128]{4,3,2,1,0:T(8,128)(2,1)S(1)} %copy-done), kind=kOutput, calls=%fused_computation.5 | convolution fusion | flops 3019898880 | bytes 69632000 | tf_op jit(solution)/shard_map/twb,tksb->tkws/dot_general | solution.py:80
  30.2 58.3 %fusion = f32[16,144,128,1]{2,0,3,1:T(8,128)S(1)} fusion(f32[40,16,128,144]{2,3,1,0:T(8,128)} %fusion.4, s32[40,16]{0,1:T(8,128)S(1)} %fusion.31, pred[40,16]{0,1:T(8,128)(4,1)S(1)} %iota_compare_fusion.1), kind=kOutput, calls=%fused_computation | convolution fusion | flops 2264944640 | bytes 48368768 | tf_op jit(solution)/shard_map/tke,tkws->ews/dot_general | solution.py:83
  88.6 0.9 constant_dynamic-update-slice_fusion.2
  89.6 2.1 %collective-permute-start.2 = (bf16[4,1,144,128]{3,2,1,0:T(8,128)(2,1)S(1)}, bf16[4,1,144,128]{3,2,1,0:T(8,128)(2,1)S(1)}, u32[]{:S(2)}, u32[]{:S(2)}) collective-permute-start(bf16[4,1,144,128]{3,2,1,0:T(8,128)(2,1)S(1)} %get-tuple-element.55), channel_id=1, source_target_pairs={{0,1},{1,2},{2,3},{3,4},{4,5},{5,6},{6,7},{7,0},{8,9},{9,10},{10,1... | collective-permute-start | bytes 442376 | tf_op jit(solution)/shard_map/ppermute | solution.py:24
  91.7 0.6 fusion.38
  92.4 1.8 %collective-permute-start.4 = (f32[4,1,144,128]{3,2,1,0:T(8,128)S(1)}, f32[4,1,144,128]{3,2,1,0:T(8,128)S(1)}, u32[]{:S(2)}, u32[]{:S(2)}) collective-permute-start(f32[4,1,144,128]{3,2,1,0:T(8,128)S(1)} %copy.20), channel_id=1, source_target_pairs={{0,1},{1,2},{2,3},{3,4},{4,5},{5,6},{6,7},{7,0},{8,9},{9,10},{10,1... | collective-permute-start | bytes 884744 | tf_op jit(solution)/shard_map/ppermute | solution.py:9
  94.2 0.3 slice.164
  94.5 0.1 copy.18
  94.6 2.0 %collective-permute-done.3 = bf16[4,1,144,128]{3,2,1,0:T(8,128)(2,1)S(1)} collective-permute-done((bf16[4,1,144,128]{3,2,1,0:T(8,128)(2,1)S(1)}, bf16[4,1,144,128]{3,2,1,0:T(8,128)(2,1)S(1)}, u32[]{:S(2)}, u32[]{:S(2)}) %collective-permute-start.3) | collective-permute-done | bytes 147488 | tf_op jit(solution)/shard_map/ppermute | solution.py:27
  96.6 0.1 pad_maximum_fusion
  96.7 10.7 %fusion.13 = bf16[40,16,144,128]{3,0,2,1:T(8,128)(2,1)} fusion(bf16[16,144,128,1]{2,1,0,3:T(8,128)(2,1)S(1)} %bitcast.61, s32[40,16]{0,1:T(8,128)S(1)} %fusion.31, pred[40,16]{0,1:T(8,128)(4,1)S(1)} %iota_compare_fusion.1), kind=kOutput, calls=%fused_computation.12 | convolution fusion | flops 377507840 | bytes 24185984 | tf_op jit(solution)/shard_map/tke,ews->tkws/dot_general | solution.py:73
  107.6 0.8 copy-done.2
  108.4 0.7 fusion.39
  109.1 2.0 %collective-permute-start.6 = (f32[1,2,144,128]{3,2,1,0:T(8,128)}, f32[1,2,144,128]{3,2,1,0:T(8,128)S(1)}, u32[]{:S(2)}, u32[]{:S(2)}) collective-permute-start(f32[1,2,144,128]{3,2,1,0:T(8,128)} %get-tuple-element.54), channel_id=1, source_target_pairs={{0,8},{8,16},{16,24},{24,32},{32,40},{40,48},{48,56},{56,64},{64,7... | collective-permute-start | bytes 442376 | tf_op jit(solution)/shard_map/ppermute | solution.py:15
  111.2 13.8 %fusion.10 = bf16[1,1,40,144,128]{4,3,2,1,0:T(8,128)(2,1)} fusion(bf16[1,1,40,16,128,128]{5,4,3,2,1,0:T(8,128)(2,1)S(1)} %bitcast.58, bf16[40,16,144,128]{3,0,2,1:T(8,128)(2,1)} %fusion.13), kind=kOutput, calls=%fused_computation.10 | convolution fusion | flops 3020636160 | bytes 46039040 | tf_op jit(solution)/shard_map/tkws,tksb->twb/dot_general | solution.py:79
  125.0 1.0 slice.169
  126.0 5.5 %collective-permute-start.7 = (f32[1,2,144,128]{3,2,1,0:T(8,128)}, f32[1,2,144,128]{3,2,1,0:T(8,128)S(1)}, u32[]{:S(2)}, u32[]{:S(2)}) collective-permute-start(f32[1,2,144,128]{3,2,1,0:T(8,128)} %get-tuple-element.53), channel_id=1, source_target_pairs={{8,0},{16,8},{24,16},{32,24},{40,32},{48,40},{56,48},{64,56},{72,6... | collective-permute-start | bytes 442376 | tf_op jit(solution)/shard_map/ppermute | solution.py:15
  131.5 0.9 fusion.18
  132.4 2.4 %collective-permute-done.7 = f32[1,2,144,128]{3,2,1,0:T(8,128)S(1)} collective-permute-done((f32[1,2,144,128]{3,2,1,0:T(8,128)}, f32[1,2,144,128]{3,2,1,0:T(8,128)S(1)}, u32[]{:S(2)}, u32[]{:S(2)}) %collective-permute-start.7) | collective-permute-done | bytes 147488 | tf_op jit(solution)/shard_map/ppermute | solution.py:15
  134.8 0.7 convert_element_type.13
  (37 shorter events, 0.3 us)
Async XLA Ops:
  0.6 6.4 %copy-start = (bf16[1,1,40,144,128]{4,3,2,1,0:T(8,128)(2,1)S(1)}, bf16[1,1,40,144,128]{4,3,2,1,0:T(8,128)(2,1)}, u32[]{:S(2)}) copy-start(bf16[1,1,40,144,128]{4,3,2,1,0:T(8,128)(2,1)} %param.14) | copy-start | bytes 4423684
  2.3 86.2 %collective-permute-start = (bf16[1,2,144,128]{3,2,1,0:T(8,128)(2,1)}, bf16[1,2,144,128]{3,2,1,0:T(8,128)(2,1)}, u32[]{:S(2)}, u32[]{:S(2)}) collective-permute-start(bf16[1,2,144,128]{3,2,1,0:T(8,128)(2,1)} %get-tuple-element.58), channel_id=1, source_target_pairs={{0,8},{8,16},{16,24},{24,32},{32,40},{40,48},{48,56},{56,64},{64,7... | collective-permute-start | bytes 221192 | tf_op jit(solution)/shard_map/ppermute | solution.py:24
  4.0 85.5 %collective-permute-start.1 = (bf16[1,2,144,128]{3,2,1,0:T(8,128)(2,1)}, bf16[1,2,144,128]{3,2,1,0:T(8,128)(2,1)S(1)}, u32[]{:S(2)}, u32[]{:S(2)}) collective-permute-start(bf16[1,2,144,128]{3,2,1,0:T(8,128)(2,1)} %get-tuple-element.57), channel_id=1, source_target_pairs={{8,0},{16,8},{24,16},{32,24},{40,32},{48,40},{56,48},{64,56},{72,6... | collective-permute-start | bytes 221192 | tf_op jit(solution)/shard_map/ppermute | solution.py:27
  7.0 23.1 %copy-start.4 = (s32[1,1,40,16]{2,3,1,0:T(8,128)S(1)}, s32[1,1,40,16]{2,3,1,0:T(8,128)}, u32[]{:S(2)}) copy-start(s32[1,1,40,16]{2,3,1,0:T(8,128)} %param.16) | copy-start | bytes 7684
  30.2 59.3 %copy-start.3 = (bf16[2,2,144,128]{3,2,1,0:T(8,128)(2,1)S(1)}, bf16[2,2,144,128]{3,2,1,0:T(8,128)(2,1)}, u32[]{:S(2)}) copy-start(bf16[2,2,144,128]{3,2,1,0:T(8,128)(2,1)} %param.13) | copy-start | bytes 442372
  30.2 80.9 %slice-start = ((s8[20971520]{0:T(1024)(128)(4,1)}), s8[4194304]{0:T(1024)(128)(4,1)S(1)}, s32[]{:S(2)}) async-start(s8[20971520]{0:T(1024)(128)(4,1)} %bitcast.57), calls=%async_computation | async-start | bytes 8388608
  30.2 80.9 %slice-start.1 = ((s8[20971520]{0:T(1024)(128)(4,1)}), s8[4194304]{0:T(1024)(128)(4,1)S(1)}, s32[]{:S(2)}) async-start(s8[20971520]{0:T(1024)(128)(4,1)} %bitcast.57), calls=%async_computation.1 | async-start | bytes 8388608
  30.2 80.9 %slice-start.2 = ((s8[20971520]{0:T(1024)(128)(4,1)}), s8[4194304]{0:T(1024)(128)(4,1)S(1)}, s32[]{:S(2)}) async-start(s8[20971520]{0:T(1024)(128)(4,1)} %bitcast.57), calls=%async_computation.2 | async-start | bytes 8388608
  89.6 5.0 %collective-permute-start.2 = (bf16[4,1,144,128]{3,2,1,0:T(8,128)(2,1)S(1)}, bf16[4,1,144,128]{3,2,1,0:T(8,128)(2,1)S(1)}, u32[]{:S(2)}, u32[]{:S(2)}) collective-permute-start(bf16[4,1,144,128]{3,2,1,0:T(8,128)(2,1)S(1)} %get-tuple-element.55), channel_id=1, source_target_pairs={{0,1},{1,2},{2,3},{3,4},{4,5},{5,6},{6,7},{7,0},{8,9},{9,10},{10,1... | collective-permute-start | bytes 442376 | tf_op jit(solution)/shard_map/ppermute | solution.py:24
  91.7 4.9 %collective-permute-start.3 = (bf16[4,1,144,128]{3,2,1,0:T(8,128)(2,1)S(1)}, bf16[4,1,144,128]{3,2,1,0:T(8,128)(2,1)S(1)}, u32[]{:S(2)}, u32[]{:S(2)}) collective-permute-start(bf16[4,1,144,128]{3,2,1,0:T(8,128)(2,1)S(1)} %get-tuple-element.56), channel_id=1, source_target_pairs={{1,0},{2,1},{3,2},{4,3},{5,4},{6,5},{7,6},{0,7},{9,8},{10,9},{11,1... | collective-permute-start | bytes 442376 | tf_op jit(solution)/shard_map/ppermute | solution.py:27
  92.3 18.8 %slice-start.3 = ((s8[20971520]{0:T(1024)(128)(4,1)}), s8[4194304]{0:T(1024)(128)(4,1)S(1)}, s32[]{:S(2)}) async-start(s8[20971520]{0:T(1024)(128)(4,1)} %bitcast.57), calls=%async_computation.3 | async-start | bytes 8388608
  92.4 15.0 %collective-permute-start.4 = (f32[4,1,144,128]{3,2,1,0:T(8,128)S(1)}, f32[4,1,144,128]{3,2,1,0:T(8,128)S(1)}, u32[]{:S(2)}, u32[]{:S(2)}) collective-permute-start(f32[4,1,144,128]{3,2,1,0:T(8,128)S(1)} %copy.20), channel_id=1, source_target_pairs={{0,1},{1,2},{2,3},{3,4},{4,5},{5,6},{6,7},{7,0},{8,9},{9,10},{10,1... | collective-permute-start | bytes 884744 | tf_op jit(solution)/shard_map/ppermute | solution.py:9
  94.2 13.3 %collective-permute-start.5 = (f32[4,1,144,128]{3,2,1,0:T(8,128)S(1)}, f32[4,1,144,128]{3,2,1,0:T(8,128)S(1)}, u32[]{:S(2)}, u32[]{:S(2)}) collective-permute-start(f32[4,1,144,128]{3,2,1,0:T(8,128)S(1)} %copy.21), channel_id=1, source_target_pairs={{0,7},{1,0},{2,1},{3,2},{4,3},{5,4},{6,5},{7,6},{8,15},{9,8},{10,9... | collective-permute-start | bytes 884744 | tf_op jit(solution)/shard_map/ppermute | solution.py:9
  96.7 14.5 %slice-start.4 = ((s8[20971520]{0:T(1024)(128)(4,1)}), s8[4194304]{0:T(1024)(128)(4,1)S(1)}, s32[]{:S(2)}) async-start(s8[20971520]{0:T(1024)(128)(4,1)} %bitcast.57), calls=%async_computation.4 | async-start | bytes 8388608
  107.5 0.8 copy-start.2
  109.1 26.4 %copy-start.1 = (bf16[1,1,40,144,128]{4,3,2,1,0:T(8,128)(2,1)S(1)}, bf16[1,1,40,144,128]{4,3,2,1,0:T(8,128)(2,1)}, u32[]{:S(2)}) copy-start(bf16[1,1,40,144,128]{4,3,2,1,0:T(8,128)(2,1)} %param.14) | copy-start | bytes 4423684
  109.1 22.4 %collective-permute-start.6 = (f32[1,2,144,128]{3,2,1,0:T(8,128)}, f32[1,2,144,128]{3,2,1,0:T(8,128)S(1)}, u32[]{:S(2)}, u32[]{:S(2)}) collective-permute-start(f32[1,2,144,128]{3,2,1,0:T(8,128)} %get-tuple-element.54), channel_id=1, source_target_pairs={{0,8},{8,16},{16,24},{24,32},{32,40},{40,48},{48,56},{56,64},{64,7... | collective-permute-start | bytes 442376 | tf_op jit(solution)/shard_map/ppermute | solution.py:15
  126.0 8.8 %collective-permute-start.7 = (f32[1,2,144,128]{3,2,1,0:T(8,128)}, f32[1,2,144,128]{3,2,1,0:T(8,128)S(1)}, u32[]{:S(2)}, u32[]{:S(2)}) collective-permute-start(f32[1,2,144,128]{3,2,1,0:T(8,128)} %get-tuple-element.53), channel_id=1, source_target_pairs={{8,0},{16,8},{24,16},{32,24},{40,32},{48,40},{56,48},{64,56},{72,6... | collective-permute-start | bytes 442376 | tf_op jit(solution)/shard_map/ppermute | solution.py:15
where the time goes:
time: 137 us; the launch traced here: 135 us
  matrix products  106 us (77%)
  starting transfers between devices  15.5 us (11%)
  local copies, waits for them, and re-layouts  6.28 us (5%)
  waiting for transfers between devices  4.33 us (3%)
  other arithmetic  2.49 us (2%)
    dot_general x1, matrix products, body(): jnp.einsum('tke,tkws->ews', selector.astype(jnp.float32), contribution, p...  58.3 us
    dot_general x1, matrix products, body(): jnp.einsum('twb,tksb->tkws', cotan_local, blocks, preferred_element_type=...  23.1 us
    dot_general x1, matrix products, body(): jnp.einsum('tkws,tksb->twb', picked, blocks, preferred_element_type=jnp.f...  13.8 us
    dot_general x1, matrix products, body(): jnp.einsum('tke,ews->tkws', selector.astype(jnp.bfloat16), flattened, pre...  10.7 us
    ppermute x2, starting transfers between devices, passed_along(): return lax.ppermute(block, axis, route)  7.52 us
    ppermute x2, starting transfers between devices, with_halo(): lax.ppermute(lax.slice_in_dim(block, block.shape[dim] - width, None, axis...  3.78 us
  transfers between devices with their start and end apart: 8, of which 2 were waited for; matrix products, arithmetic and copies ran while one was open for 82% of the time, Pallas kernels for 0%

commit v1 on v0

v1 whole, which is shorter than its diff:
```python
import jax
import jax.numpy as jnp
from jax import lax
from jax.experimental import pallas as pl
from jax.experimental.pallas import tpu as pltpu
from jax.sharding import PartitionSpec as P

W, B, S = 144, 128, 128
TB, KPT = 40, 16
STEP = 2


def ring(value, axis, by):
    n = lax.axis_size(axis)
    return lax.ppermute(value, axis, [(i, (i + by) % n) for i in range(n)])


def line(value, axis, by):
    n = lax.axis_size(axis)
    return lax.ppermute(value, axis, [(i, i + by) for i in range(n) if 0 <= i + by < n])


def adjoint_kernel(pos_ref, cot_ref, w_ref, west, east, north, south, inner, acc):
    step = pl.program_id(0)

    @pl.when(step == 0)
    def _():
        acc[...] = jnp.zeros_like(acc)

    for u in range(STEP):
        t = step * STEP + u
        wt = w_ref[u].reshape(KPT * S, B)
        out = lax.dot_general(
            cot_ref[u], wt, (((1,), (1,)), ((), ())), preferred_element_type=jnp.float32
        )
        for k in range(KPT):
            e = pos_ref[t * KPT + k]
            acc[e] = acc[e] + out[:, k * S:(k + 1) * S]

    @pl.when(step == pl.num_programs(0) - 1)
    def _():
        for r in range(4):
            west[r] = acc[4 * r]
            east[r] = acc[4 * r + 3]
        for c in range(2):
            north[c] = acc[1 + c]
            south[c] = acc[13 + c]
            inner[0, c] = acc[5 + c]
            inner[1, c] = acc[9 + c]


def adjoint(pos, cot, weights):
    block = lambda *s: jax.ShapeDtypeStruct(s + (W, S), jnp.float32)
    whole = lambda *s: pl.BlockSpec(s + (W, S), lambda i, p: (0,) * (len(s) + 2))
    return pl.pallas_call(
        adjoint_kernel,
        grid_spec=pltpu.PrefetchScalarGridSpec(
            num_scalar_prefetch=1,
            grid=(TB // STEP,),
            in_specs=[
                pl.BlockSpec((STEP, W, B), lambda i, p: (i, 0, 0)),
                pl.BlockSpec((STEP, KPT, S, B), lambda i, p: (i, 0, 0, 0)),
            ],
            out_specs=[whole(4), whole(4), whole(2), whole(2), whole(2, 2)],
            scratch_shapes=[pltpu.VMEM((17, W, S), jnp.float32)],
        ),
        out_shape=[block(4), block(4), block(2), block(2), block(2, 2)],
        cost_estimate=pl.CostEstimate(flops=2 * TB * KPT * W * S * B, bytes_accessed=TB * KPT * S * B * 2, transcendentals=0),
        name="adjoint",
    )(pos, cot, weights)


def forward_kernel(pos_ref, own, nb, sb, wb, eb, w_ref, prev, out_ref, ext, sem, *, first):
    step = pl.program_id(0)

    @pl.when(step == 0)
    def _():
        moves = [(wb, slice(0, 4), None)]
        copies = []
        for r in range(4):
            copies.append((wb.at[r], ext.at[4 * r]))
            copies.append((eb.at[r], ext.at[4 * r + 3]))
        for c in range(2):
            copies.append((nb.at[c], ext.at[1 + c]))
            copies.append((sb.at[c], ext.at[13 + c]))
            copies.append((own.at[0, c], ext.at[5 + c]))
            copies.append((own.at[1, c], ext.at[9 + c]))
        for s, d in copies:
            pltpu.make_async_copy(s, d, sem).start()
        ext[16] = jnp.zeros((W, S), jnp.bfloat16)
        for s, d in copies:
            pltpu.make_async_copy(s, d, sem).wait()

    for u in range(STEP):
        t = (step + first) * STEP + u
        lhs = jnp.concatenate([ext[pos_ref[t * KPT + k]] for k in range(KPT)], axis=1)
        wt = w_ref[u].reshape(KPT * S, B)
        out = jnp.dot(lhs, wt, preferred_element_type=jnp.float32)
        out_ref[u] = out.astype(jnp.bfloat16)


def forward(pos, own, nb, sb, wb, eb, weights, prev, first, count):
    import functools
    anyspec = pl.BlockSpec(memory_space=pl.ANY)
    args = [pos, own, nb, sb, wb, eb, weights]
    in_specs = [anyspec] * 5 + [pl.BlockSpec((STEP, KPT, S, B), lambda i, p: (i + first, 0, 0, 0))]
    body = functools.partial(forward_kernel, first=first)
    if prev is None:
        body_fn = lambda p, a, b, c, d, e, w, o, x, s: body(p, a, b, c, d, e, w, None, o, x, s)
        alias = {}
    else:
        body_fn = body
        args.append(prev)
        in_specs.append(anyspec)
        alias = {7: 0}
    return pl.pallas_call(
        body_fn,
        grid_spec=pltpu.PrefetchScalarGridSpec(
            num_scalar_prefetch=1,
            grid=(count,),
            in_specs=in_specs,
            out_specs=pl.BlockSpec((STEP, W, B), lambda i, p: (i + first, 0, 0)),
            scratch_shapes=[pltpu.VMEM((17, W, S), jnp.bfloat16), pltpu.SemaphoreType.DMA],
        ),
        out_shape=jax.ShapeDtypeStruct((TB, W, B), jnp.bfloat16),
        input_output_aliases=alias,
        cost_estimate=pl.CostEstimate(flops=2 * count * STEP * KPT * W * S * B, bytes_accessed=count * STEP * KPT * S * B * 2, transcendentals=0),
        name="forward",
    )(*args)


def body(increment, cotangent, weights, source_ids, counts):
    side = increment.shape[0]
    cols = side * lax.axis_size("lon")
    ids = source_ids[0, 0]
    row = ids // cols - lax.axis_index("lat") * side + 1
    col = (ids % cols - lax.axis_index("lon") * side + 1 + cols) % cols
    live = jnp.arange(KPT, dtype=jnp.int32)[None, :] < counts[0, 0][:, None]
    pos = jnp.where(live, row * 4 + col, 16).astype(jnp.int32).reshape(-1)
    w = weights[0, 0]

    nb = line(increment[1:2], "lat", 1)[0]
    sb = line(increment[0:1], "lat", -1)[0]
    column = lambda c: jnp.concatenate([nb[c][None], increment[:, c], sb[c][None]])
    wb = ring(column(1), "lon", 1)
    eb = ring(column(0), "lon", -1)

    west, east, north, south, inner = adjoint(pos, cotangent[0, 0], w)
    fw = ring(east, "lon", 1)
    fe = ring(west, "lon", -1)
    ocean = forward(pos, increment, nb, sb, wb, eb, w, None, 0, 8)
    lon_in = jnp.stack([fw, fe], axis=1)
    fn = line(south + lon_in[3], "lat", 1)
    fs = line(north + lon_in[0], "lat", -1)
    ocean = forward(pos, increment, nb, sb, wb, eb, w, ocean, 8, 12)
    total = inner + lon_in[1:3] + jnp.stack([fn, fs])
    return ocean[None, None], total.astype(jnp.bfloat16)


def solution(mesh):
    placed = (
        P("lat", "lon", None, None),
        P("lat", "lon", None, None, None),
        P("lat", "lon", None, None, None, None),
        P("lat", "lon", None, None),
        P("lat", "lon", None),
    )
    return jax.shard_map(
        body,
        mesh=mesh,
        in_specs=placed,
        out_specs=(P("lat", "lon", None, None, None), P("lat", "lon", None, None)),
        check_vma=False,
    )
```

time: 137 us -> 75.4 us (0.55)
  matrix products: 106 us -> 0 us
  Pallas kernels: 0 us -> 45.1 us
  local copies, waits for them, and re-layouts: 6.28 us -> 2.57 us
  starting transfers between devices: 15.5 us -> 17.5 us
  waiting for transfers between devices: 4.33 us -> 6.03 us
    dot_general x4 -> x0, matrix products: 106 us -> none  [the longest x1 58.3 us: body(): jnp.einsum('tke,tkws->ews', selector.astype(jnp.float32), contribution, p...]
    pallas_call x0 -> x3, Pallas kernels: none -> 45.1 us  [the longest x2 24 us: forward(): pl.pallas_call(body_fn, grid_spec=pltpu.PrefetchScalarGridSpec(num_scalar...]
    slice x6 -> x3, local copies, waits for them, and re-layouts: 4.33 us -> 0.95 us  [the longest x1 0.93 us: body(): sb = line(increment[0:1], 'lat', -1)[0]]
    ppermute x8, starting transfers between devices: 15.5 us -> 17.5 us  [the longest x4 13.6 us: line(): lax.ppermute(value, axis, [(i, i + by) for i in range(n) if 0 <= i + by <...]
    ppermute x8, waiting for transfers between devices: 4.33 us -> 6.03 us  [the longest x4 6.02 us: ring(): return lax.ppermute(value, axis, [(i, (i + by) % n) for i in range(n)])]
  transfers between devices with their start and end apart: 8 -> 8, of which waited for: 2 -> 2; matrix products, arithmetic and copies ran while one was open for 82% -> 3% of each run, Pallas kernels for 0% -> 61%
where the time goes in v1:
time: 75.4 us; the launch traced here: 74.1 us
  Pallas kernels  45.1 us (60%)
  starting transfers between devices  17.5 us (23%)
  waiting for transfers between devices  6.03 us (8%)
  local copies, waits for them, and re-layouts  2.57 us (3%)
  other arithmetic  2.13 us (3%)
  between operations  0.84 us (1%)
    pallas_call x2, Pallas kernels, forward(): pl.pallas_call(body_fn, grid_spec=pltpu.PrefetchScalarGridSpec(num_scalar...  24 us
    pallas_call x1, Pallas kernels, adjoint(): pl.pallas_call(adjoint_kernel, grid_spec=pltpu.PrefetchScalarGridSpec(num...  21.1 us
    ppermute x4, starting transfers between devices, line(): lax.ppermute(value, axis, [(i, i + by) for i in range(n) if 0 <= i + by <...  13.6 us
    ppermute x4, waiting for transfers between devices, ring(): return lax.ppermute(value, axis, [(i, (i + by) % n) for i in range(n)])  6.02 us
    ppermute x4, starting transfers between devices, ring(): return lax.ppermute(value, axis, [(i, (i + by) % n) for i in range(n)])  3.89 us
  transfers between devices with their start and end apart: 8, of which 2 were waited for; matrix products, arithmetic and copies ran while one was open for 3% of the time, Pallas kernels for 61%

profile of v1, /device:TPU:15, one launch (start us, length us, event | category | flops | bytes accessed | tf_op | source)
XLA Modules:
  0.0 74.1 jit_solution(14947370867124060837)
XLA Ops:
  0.6 0.9 %fusion.19 = (bf16[1,2,144,128]{3,2,1,0:T(8,128)(2,1)S(1)}, bf16[1,2,144,128]{3,2,1,0:T(8,128)(2,1)S(1)}) fusion(bf16[2,2,144,128]{3,2,1,0:T(8,128)(2,1)} %own.1), kind=kLoop, calls=%fused_computation.42 | loop fusion | bytes 294912 | tf_op jit(solution)/shard_map/slice | solution.py:143
  1.6 3.5 %collective-permute-start = (bf16[1,2,144,128]{3,2,1,0:T(8,128)(2,1)S(1)}, bf16[1,2,144,128]{3,2,1,0:T(8,128)(2,1)S(1)}, u32[]{:S(2)}, u32[]{:S(2)}) collective-permute-start(bf16[1,2,144,128]{3,2,1,0:T(8,128)(2,1)S(1)} %get-tuple-element.17), channel_id=1, source_target_pairs={{0,8},{8,16},{16,24},{24,32},{32,40},{40,48},{48,56},{56,64},{64,7... | collective-permute-start | bytes 221192 | tf_op jit(solution)/shard_map/ppermute | solution.py:20
  5.1 4.3 %collective-permute-start.1 = (bf16[1,2,144,128]{3,2,1,0:T(8,128)(2,1)S(1)}, bf16[1,2,144,128]{3,2,1,0:T(8,128)(2,1)S(1)}, u32[]{:S(2)}, u32[]{:S(2)}) collective-permute-start(bf16[1,2,144,128]{3,2,1,0:T(8,128)(2,1)S(1)} %get-tuple-element.16), channel_id=1, source_target_pairs={{8,0},{16,8},{24,16},{32,24},{40,32},{48,40},{56,48},{64,56},{72,6... | collective-permute-start | bytes 221192 | tf_op jit(solution)/shard_map/ppermute | solution.py:20
  9.4 0.7 iota_compare_fusion
  10.2 0.1 lt.33
  10.3 0.8 %copy.10 = s32[1,1,40,16]{3,2,1,0:T(8,128)S(1)} copy(s32[1,1,40,16]{2,3,1,0:T(8,128)} %param.8) | data formatting | bytes 5120 | tf_op args[3]
  11.0 0.1 squeeze.27
  11.1 0.6 fusion.13.p.pos_ref
  11.7 21.1 %adjoint.1 = (f32[4,144,128]{2,1,0:T(8,128)}, f32[4,144,128]{2,1,0:T(8,128)}, f32[2,144,128]{2,1,0:T(8,128)}, f32[2,144,128]{2,1,0:T(8,128)}, f32[2,2,144,128]{3,2,1,0:T(8,128)}) custom-call(s32[640]{0:T(1024)} %fusion.13.p.pos_ref, bf16[40,144,128]{2,1,0:T(8,128)(2,1)} %bitcast.40, bf16[40,16,128,128]{3,2,1,0:T(8,128)(2,1)} %bitcast.36), custom_call_target="tpu_custom_call" | custom-call | flops 3019898880 | bytes 20971520 | tf_op jit(solution)/shard_map/adjoint/pallas_call | solution.py:55
  32.8 2.1 %collective-permute-start.4 = (f32[4,144,128]{2,1,0:T(8,128)}, f32[4,144,128]{2,1,0:T(8,128)S(1)}, u32[]{:S(2)}, u32[]{:S(2)}) collective-permute-start(f32[4,144,128]{2,1,0:T(8,128)} %get-tuple-element.8), channel_id=1, source_target_pairs={{0,1},{1,2},{2,3},{3,4},{4,5},{5,6},{6,7},{7,0},{8,9},{9,10},{10,1... | collective-permute-start | bytes 884744 | tf_op jit(solution)/shard_map/ppermute | solution.py:15
  35.0 0.0 collective-permute-done.1
  35.0 0.0 collective-permute-done
  35.1 1.8 %collective-permute-start.2 = (bf16[4,144,128]{2,1,0:T(8,128)(2,1)S(1)}, bf16[4,144,128]{2,1,0:T(8,128)(2,1)S(1)}, u32[]{:S(2)}, u32[]{:S(2)}) collective-permute-start(bf16[4,144,128]{2,1,0:T(8,128)(2,1)S(1)} %pad_maximum_fusion.1), channel_id=1, source_target_pairs={{0,1},{1,2},{2,3},{3,4},{4,5},{5,6},{6,7},{7,0},{8,9},{9,10},{10,1... | collective-permute-start | bytes 442376 | tf_op jit(solution)/shard_map/ppermute | solution.py:15
  36.9 0.0 collective-permute-start.3
  36.9 3.5 %collective-permute-done.2.d.wb = bf16[4,144,128]{2,1,0:T(8,128)(2,1)S(1)} collective-permute-done((bf16[4,144,128]{2,1,0:T(8,128)(2,1)S(1)}, bf16[4,144,128]{2,1,0:T(8,128)(2,1)S(1)}, u32[]{:S(2)}, u32[]{:S(2)}) %collective-permute-start.2) | collective-permute-done | bytes 147488 | tf_op jit(solution)/shard_map/ppermute | solution.py:15
  40.4 2.5 %collective-permute-done.3.e.eb = bf16[4,144,128]{2,1,0:T(8,128)(2,1)S(1)} collective-permute-done((bf16[4,144,128]{2,1,0:T(8,128)(2,1)S(1)}, bf16[4,144,128]{2,1,0:T(8,128)(2,1)S(1)}, u32[]{:S(2)}, u32[]{:S(2)}) %collective-permute-start.3) | collective-permute-done | bytes 147488 | tf_op jit(solution)/shard_map/ppermute | solution.py:15
  42.9 0.6 copy-done.4
  43.5 10.2 %forward.2.prev = bf16[40,144,128]{2,1,0:T(8,128)(2,1)} custom-call(s32[640]{0:T(1024)} %fusion.13.p.pos_ref, bf16[2,2,144,128]{3,2,1,0:T(8,128)(2,1)} %own.1, bf16[2,144,128]{2,1,0:T(8,128)(2,1)} %bitcast.45, bf16[2,144,128]{2,1,0:T(8,128)(2,1)} %bitcast.47, bf16[4,144,128]{2,1,0:T(8,128)(2,1)} %copy-done.3, bf16[4,144,128]{2,1,0:T(8,128)(2,1)} %copy-done.4, ...), custom_call_target="tpu_custom_call" | custom-call | flops 1207959552 | bytes 8388608 | tf_op jit(solution)/shard_map/forward/pallas_call | solution.py:116
  53.8 0.0 collective-permute-done.4
  53.9 3.7 %collective-permute-start.7 = (f32[2,144,128]{2,1,0:T(8,128)S(1)}, f32[2,144,128]{2,1,0:T(8,128)S(1)}, u32[]{:S(2)}, u32[]{:S(2)}) collective-permute-start(f32[2,144,128]{2,1,0:T(8,128)S(1)} %get-tuple-element.13), channel_id=1, source_target_pairs={{8,0},{16,8},{24,16},{32,24},{40,32},{48,40},{56,48},{64,56},{72,6... | collective-permute-start | bytes 442376 | tf_op jit(solution)/shard_map/ppermute | solution.py:20
  57.5 2.1 %collective-permute-start.6 = (f32[2,144,128]{2,1,0:T(8,128)S(1)}, f32[2,144,128]{2,1,0:T(8,128)S(1)}, u32[]{:S(2)}, u32[]{:S(2)}) collective-permute-start(f32[2,144,128]{2,1,0:T(8,128)S(1)} %get-tuple-element.12), channel_id=1, source_target_pairs={{0,8},{8,16},{16,24},{24,32},{32,40},{40,48},{48,56},{56,64},{64,7... | collective-permute-start | bytes 442376 | tf_op jit(solution)/shard_map/ppermute | solution.py:20
  59.6 13.7 %forward.3 = bf16[40,144,128]{2,1,0:T(8,128)(2,1)} custom-call(s32[640]{0:T(1024)} %fusion.13.p.pos_ref, bf16[2,2,144,128]{3,2,1,0:T(8,128)(2,1)} %own.1, bf16[2,144,128]{2,1,0:T(8,128)(2,1)} %bitcast.46, bf16[2,144,128]{2,1,0:T(8,128)(2,1)} %bitcast.48, bf16[4,144,128]{2,1,0:T(8,128)(2,1)} %copy-done.3, ...), custom_call_target="tpu_custom_call", output_to_operand_aliasing={{}: (7, {})} | custom-call | flops 1811939328 | bytes 12582912 | tf_op jit(solution)/shard_map/forward/pallas_call | solution.py:116
  73.4 0.0 collective-permute-done.7
  73.4 0.7 fusion.3
  (24 shorter events, 0.1 us)
Async XLA Ops:
  1.6 33.4 %collective-permute-start = (bf16[1,2,144,128]{3,2,1,0:T(8,128)(2,1)S(1)}, bf16[1,2,144,128]{3,2,1,0:T(8,128)(2,1)S(1)}, u32[]{:S(2)}, u32[]{:S(2)}) collective-permute-start(bf16[1,2,144,128]{3,2,1,0:T(8,128)(2,1)S(1)} %get-tuple-element.17), channel_id=1, source_target_pairs={{0,8},{8,16},{16,24},{24,32},{32,40},{40,48},{48,56},{56,64},{64,7... | collective-permute-start | bytes 221192 | tf_op jit(solution)/shard_map/ppermute | solution.py:20
  5.1 29.9 %collective-permute-start.1 = (bf16[1,2,144,128]{3,2,1,0:T(8,128)(2,1)S(1)}, bf16[1,2,144,128]{3,2,1,0:T(8,128)(2,1)S(1)}, u32[]{:S(2)}, u32[]{:S(2)}) collective-permute-start(bf16[1,2,144,128]{3,2,1,0:T(8,128)(2,1)S(1)} %get-tuple-element.16), channel_id=1, source_target_pairs={{8,0},{16,8},{24,16},{32,24},{40,32},{48,40},{56,48},{64,56},{72,6... | collective-permute-start | bytes 221192 | tf_op jit(solution)/shard_map/ppermute | solution.py:20
  11.7 23.2 %copy-start = (bf16[2,2,144,128]{3,2,1,0:T(8,128)(2,1)S(1)}, bf16[2,2,144,128]{3,2,1,0:T(8,128)(2,1)}, u32[]{:S(2)}) copy-start(bf16[2,2,144,128]{3,2,1,0:T(8,128)(2,1)} %own.1) | copy-start | bytes 442372
  32.8 21.0 %collective-permute-start.4 = (f32[4,144,128]{2,1,0:T(8,128)}, f32[4,144,128]{2,1,0:T(8,128)S(1)}, u32[]{:S(2)}, u32[]{:S(2)}) collective-permute-start(f32[4,144,128]{2,1,0:T(8,128)} %get-tuple-element.8), channel_id=1, source_target_pairs={{0,1},{1,2},{2,3},{3,4},{4,5},{5,6},{6,7},{7,0},{8,9},{9,10},{10,1... | collective-permute-start | bytes 884744 | tf_op jit(solution)/shard_map/ppermute | solution.py:15
  35.0 18.8 %collective-permute-start.5 = (f32[4,144,128]{2,1,0:T(8,128)}, f32[4,144,128]{2,1,0:T(8,128)S(1)}, u32[]{:S(2)}, u32[]{:S(2)}) collective-permute-start(f32[4,144,128]{2,1,0:T(8,128)} %get-tuple-element.9), channel_id=1, source_target_pairs={{0,7},{1,0},{2,1},{3,2},{4,3},{5,4},{6,5},{7,6},{8,15},{9,8},{10,9... | collective-permute-start | bytes 884744 | tf_op jit(solution)/shard_map/ppermute | solution.py:15
  35.0 7.9 %copy-start.2 = (bf16[1,2,144,128]{3,2,1,0:T(8,128)(2,1)}, bf16[1,2,144,128]{3,2,1,0:T(8,128)(2,1)S(1)}, u32[]{:S(2)}) copy-start(bf16[1,2,144,128]{3,2,1,0:T(8,128)(2,1)S(1)} %collective-permute-done.1) | copy-start | bytes 221188
  35.0 7.9 %copy-start.1 = (bf16[1,2,144,128]{3,2,1,0:T(8,128)(2,1)}, bf16[1,2,144,128]{3,2,1,0:T(8,128)(2,1)S(1)}, u32[]{:S(2)}) copy-start(bf16[1,2,144,128]{3,2,1,0:T(8,128)(2,1)S(1)} %collective-permute-done) | copy-start | bytes 221188
  35.1 5.3 %collective-permute-start.2 = (bf16[4,144,128]{2,1,0:T(8,128)(2,1)S(1)}, bf16[4,144,128]{2,1,0:T(8,128)(2,1)S(1)}, u32[]{:S(2)}, u32[]{:S(2)}) collective-permute-start(bf16[4,144,128]{2,1,0:T(8,128)(2,1)S(1)} %pad_maximum_fusion.1), channel_id=1, source_target_pairs={{0,1},{1,2},{2,3},{3,4},{4,5},{5,6},{6,7},{7,0},{8,9},{9,10},{10,1... | collective-permute-start | bytes 442376 | tf_op jit(solution)/shard_map/ppermute | solution.py:15
  36.9 6.0 %collective-permute-start.3 = (bf16[4,144,128]{2,1,0:T(8,128)(2,1)S(1)}, bf16[4,144,128]{2,1,0:T(8,128)(2,1)S(1)}, u32[]{:S(2)}, u32[]{:S(2)}) collective-permute-start(bf16[4,144,128]{2,1,0:T(8,128)(2,1)S(1)} %pad_maximum_fusion.2), channel_id=1, source_target_pairs={{0,7},{1,0},{2,1},{3,2},{4,3},{5,4},{6,5},{7,6},{8,15},{9,8},{10,9... | collective-permute-start | bytes 442376 | tf_op jit(solution)/shard_map/ppermute | solution.py:15
  40.4 2.5 %copy-start.3 = (bf16[4,144,128]{2,1,0:T(8,128)(2,1)}, bf16[4,144,128]{2,1,0:T(8,128)(2,1)S(1)}, u32[]{:S(2)}) copy-start(bf16[4,144,128]{2,1,0:T(8,128)(2,1)S(1)} %collective-permute-done.2.d.wb) | copy-start | bytes 442372
  42.9 0.7 copy-start.4
  43.5 10.3 %copy-start.6 = (f32[2,144,128]{2,1,0:T(8,128)S(1)}, f32[2,144,128]{2,1,0:T(8,128)}, u32[]{:S(2)}) copy-start(f32[2,144,128]{2,1,0:T(8,128)} %get-tuple-element.11) | copy-start | bytes 442372
  43.5 10.3 %copy-start.7 = (f32[2,144,128]{2,1,0:T(8,128)S(1)}, f32[2,144,128]{2,1,0:T(8,128)}, u32[]{:S(2)}) copy-start(f32[2,144,128]{2,1,0:T(8,128)} %get-tuple-element.10) | copy-start | bytes 442372
  53.9 19.5 %collective-permute-start.7 = (f32[2,144,128]{2,1,0:T(8,128)S(1)}, f32[2,144,128]{2,1,0:T(8,128)S(1)}, u32[]{:S(2)}, u32[]{:S(2)}) collective-permute-start(f32[2,144,128]{2,1,0:T(8,128)S(1)} %get-tuple-element.13), channel_id=1, source_target_pairs={{8,0},{16,8},{24,16},{32,24},{40,32},{48,40},{56,48},{64,56},{72,6... | collective-permute-start | bytes 442376 | tf_op jit(solution)/shard_map/ppermute | solution.py:20
  57.5 15.8 %copy-start.5 = (f32[2,2,144,128]{3,2,1,0:T(8,128)S(1)}, f32[2,2,144,128]{3,2,1,0:T(8,128)}, u32[]{:S(2)}) copy-start(f32[2,2,144,128]{3,2,1,0:T(8,128)} %get-tuple-element.7) | copy-start | bytes 884740
  57.5 15.8 %collective-permute-start.6 = (f32[2,144,128]{2,1,0:T(8,128)S(1)}, f32[2,144,128]{2,1,0:T(8,128)S(1)}, u32[]{:S(2)}, u32[]{:S(2)}) collective-permute-start(f32[2,144,128]{2,1,0:T(8,128)S(1)} %get-tuple-element.12), channel_id=1, source_target_pairs={{0,8},{8,16},{16,24},{24,32},{32,40},{40,48},{48,56},{56,64},{64,7... | collective-permute-start | bytes 442376 | tf_op jit(solution)/shard_map/ppermute | solution.py:20
